TPU v7x, 32 devices: a whole 2x2x4 slice. The times are simulated.
32 devices in a mesh: row: 16 (over z, y, core), col: 2 (over x).
Axes of the slice: x: 2, y: 2, z: 4, core: 2. Of those that a mesh axis runs over, the one named last changes fastest.
Arguments:
- pair_act: bfloat16 [192, 192, 128], P('row', 'col'), may hold values from -6 to 6
- tile_mask: int32 [12, 12], replicated, may hold values 0 or 1
- w_left_gate: bfloat16 [128, 128], replicated, may hold values from -0.5 to 0.5
- w_left: bfloat16 [128, 128], replicated, may hold values from -0.5 to 0.5
- w_right_gate: bfloat16 [128, 128], replicated, may hold values from -0.5 to 0.5
- w_right: bfloat16 [128, 128], replicated, may hold values from -0.5 to 0.5
- w_out_gate: bfloat16 [128, 128], replicated, may hold values from -0.5 to 0.5
- w_out: bfloat16 [128, 128], replicated, may hold values from -0.5 to 0.5
Outputs:
- update: bfloat16 [192, 192, 128], P('row', 'col')
All inputs are finite; a program needn't handle non-finite values.
Results may differ from a plain program's by a relative error of at most 0.0083.
Values may be sent and summed in bfloat16 or wider, within the bound.
A program may use at most 64 MiB of HBM per device.

v0:
```python
import jax
import jax.numpy as jnp
from jax import lax
from jax.sharding import PartitionSpec as P

TILES = 12


def norm_axis(values, axis):
    mean = jnp.mean(values, axis=axis, keepdims=True)
    centred = values - mean
    spread = jnp.mean(centred * centred, axis=axis, keepdims=True)
    return centred * lax.rsqrt(spread + 1e-05)


def local(pair_act, tile_mask, w_left_gate, w_left, w_right_gate, w_right, w_out_gate, w_out):
    rows, cols, width = pair_act.shape
    residues = rows * lax.axis_size("row")
    tile = residues // TILES
    normed = norm_axis(pair_act.astype(jnp.float32), 2).astype(jnp.bfloat16)
    tile_range = lax.iota(jnp.int32, TILES)
    row_ids = (lax.axis_index("row") * rows + lax.iota(jnp.int32, rows)) // tile
    col_ids = (lax.axis_index("col") * cols + lax.iota(jnp.int32, cols)) // tile
    row_hot = (row_ids[:, None] == tile_range[None, :]).astype(jnp.float32)
    col_hot = (col_ids[:, None] == tile_range[None, :]).astype(jnp.float32)
    pair_mask = jnp.dot(
        jnp.dot(row_hot, tile_mask.astype(jnp.float32), preferred_element_type=jnp.float32),
        col_hot.T,
        preferred_element_type=jnp.float32,
    )

    def project(weight):
        return jnp.einsum("ijd,de->eij", normed, weight, preferred_element_type=jnp.float32)

    left = (jax.nn.sigmoid(project(w_left_gate)) * project(w_left) * pair_mask[None]).astype(
        jnp.bfloat16
    )
    right = (jax.nn.sigmoid(project(w_right_gate)) * project(w_right) * pair_mask[None]).astype(
        jnp.bfloat16
    )
    left_rows, right_rows = (
        lax.all_to_all(left, "row", split_axis=0, concat_axis=1, tiled=True),
        lax.all_to_all(right, "row", split_axis=0, concat_axis=1, tiled=True),
    )
    right_block = lax.all_to_all(right_rows, "col", split_axis=1, concat_axis=2, tiled=True)
    triangle = jnp.einsum(
        "cik,cjk->jci",
        lax.all_gather(left_rows, "col", axis=2, tiled=True),
        right_block,
        preferred_element_type=jnp.float32,
    )
    triangle = triangle.astype(jnp.bfloat16)
    owned = lax.all_to_all(triangle, "row", split_axis=2, concat_axis=1, tiled=True)
    scaled = norm_axis(owned.astype(jnp.float32), 1).astype(jnp.bfloat16)
    projected = jnp.einsum("jci,ce->ije", scaled, w_out, preferred_element_type=jnp.float32)
    gate = jax.nn.sigmoid(
        jnp.einsum("ijd,de->ije", normed, w_out_gate, preferred_element_type=jnp.float32)
    )
    return (gate * projected).astype(jnp.bfloat16)


def solution(mesh):
    return jax.shard_map(
        local,
        mesh=mesh,
        in_specs=(P("row", "col", None), P(), P(), P(), P(), P(), P(), P()),
        out_specs=P("row", "col", None),
        check_vma=False,
    )
```

profile of v0, /device:TPU:0, one launch (start us, length us, event | category | flops | bytes accessed | tf_op | source)
XLA Modules:
  0.0 84.8 jit_solution(9804419726071187752)
XLA Ops:
  0.0 0.0 copy-start
  0.0 0.0 copy-start.1
  0.0 1.2 %convert_reduce_fusion = f32[12,96]{1,0:T(8,128)S(1)} fusion(bf16[12,96,128]{2,1,0:T(8,128)(2,1)} %param.8), kind=kLoop, calls=%fused_computation.34 | loop fusion | flops 293760 | bytes 299520 | tf_op jit(solution)/shard_map/reduce_sum | solution.py:10
  1.2 0.0 copy-done.1
  1.2 0.5 fusion.26
  1.7 0.0 copy-done
  1.7 0.0 copy-start.7
  1.7 0.8 fusion.8
  2.5 0.0 copy-done.7
  2.5 0.0 copy-start.2
  2.5 0.3 fusion.18
  2.8 0.5 copy-done.2
  3.3 0.5 fusion.17
  3.8 1.2 %copy.22 = bf16[128,12,96]{2,1,0:T(8,128)(2,1)} copy(bf16[128,12,96]{0,2,1:T(8,128)(2,1)S(1)} %fusion.17) | data formatting | bytes 589824 | tf_op jit(solution)/shard_map/convert_element_type | solution.py:38
  5.0 0.0 copy-start.5
  5.0 7.5 %all-to-all-start = ((bf16[128,12,96]{2,1,0:T(8,128)(2,1)}), bf16[128,12,96]{2,1,0:T(8,128)(2,1)S(1)}, u32[]{:S(2)}, u32[]{:S(2)}) async-start(bf16[128,12,96]{2,1,0:T(8,128)(2,1)} %copy.22), calls=%async_computation | async-start | bytes 1048576 | tf_op jit(solution)/shard_map/all_to_all | solution.py:43
  12.6 0.0 copy-done.5
  12.6 0.0 copy-start.3
  12.6 0.8 fusion.5
  13.4 0.0 copy-done.3
  13.4 0.5 fusion.16
  13.9 1.2 %copy.27 = bf16[128,12,96]{2,1,0:T(8,128)(2,1)} copy(bf16[128,12,96]{0,2,1:T(8,128)(2,1)S(1)} %fusion.16) | data formatting | bytes 589824 | tf_op jit(solution)/shard_map/convert_element_type | solution.py:35
  15.1 11.7 %all-to-all-done = bf16[128,12,96]{2,1,0:T(8,128)(2,1)S(1)} async-done(((bf16[128,12,96]{2,1,0:T(8,128)(2,1)}), bf16[128,12,96]{2,1,0:T(8,128)(2,1)S(1)}, u32[]{:S(2)}, u32[]{:S(2)}) %all-to-all-start) | async-done | bytes 294944 | tf_op jit(solution)/shard_map/all_to_all | solution.py:43
  26.8 4.2 %all-to-all-start.2 = ((bf16[128,12,96]{2,1,0:T(8,128)(2,1)}), bf16[128,12,96]{2,1,0:T(8,128)(2,1)S(1)}, u32[]{:S(2)}, u32[]{:S(2)}) async-start(bf16[128,12,96]{2,1,0:T(8,128)(2,1)} %copy.27), calls=%async_computation.2 | async-start | bytes 1048576 | tf_op jit(solution)/shard_map/all_to_all | solution.py:42
  31.0 0.8 copy.24
  31.9 13.4 %all-to-all-done.2 = bf16[128,12,96]{2,1,0:T(8,128)(2,1)S(1)} async-done(((bf16[128,12,96]{2,1,0:T(8,128)(2,1)}), bf16[128,12,96]{2,1,0:T(8,128)(2,1)S(1)}, u32[]{:S(2)}, u32[]{:S(2)}) %all-to-all-start.2) | async-done | bytes 294944 | tf_op jit(solution)/shard_map/all_to_all | solution.py:42
  45.3 3.5 %all-to-all-start.1 = ((bf16[8,192,96]{2,0,1:T(8,128)(2,1)}), bf16[8,192,96]{2,0,1:T(8,128)(2,1)S(1)}, u32[]{:S(2)}, u32[]{:S(2)}) async-start(bf16[8,192,96]{2,0,1:T(8,128)(2,1)} %bitcast.7), calls=%async_computation.1 | async-start | bytes 786432 | tf_op jit(solution)/shard_map/all_to_all | solution.py:45
  48.8 0.1 copy.29
  48.9 0.4 copy.30
  49.3 15.0 %all_gather.3 = bf16[8,192,192]{1,0,2:T(8,128)(2,1)S(1)} all-gather(bf16[8,192,96]{1,0,2:T(8,128)(2,1)S(1)} %copy.30), channel_id=1, replica_groups=mesh['row'=16,'col'=2] {'col'}, dimensions={2}, use_global_device_ids=true | all-gather | bytes 884736 | tf_op jit(solution)/shard_map/all_gather | solution.py:48
  64.3 0.0 all-to-all-done.1
  64.3 0.4 copy.26
  64.7 0.2 all_to_all.53
  65.0 0.3 fusion.15
  65.3 1.0 %copy.32 = bf16[96,8,192]{0,1,2:T(8,128)(2,1)} copy(bf16[96,8,192]{2,0,1:T(8,128)(2,1)S(1)} %fusion.15) | data formatting | bytes 589824 | tf_op jit(solution)/shard_map/convert_element_type | solution.py:52
  66.2 0.0 copy-start.6
  66.2 4.5 %all-to-all-start.3 = ((bf16[96,8,192]{0,1,2:T(8,128)(2,1)}), bf16[96,8,192]{0,1,2:T(8,128)(2,1)S(1)}, u32[]{:S(2)}, u32[]{:S(2)}) async-start(bf16[96,8,192]{0,1,2:T(8,128)(2,1)} %copy.32), calls=%async_computation.3 | async-start | bytes 786432 | tf_op jit(solution)/shard_map/all_to_all | solution.py:53
  70.8 0.0 copy-done.6
  70.8 0.8 fusion.11
  71.6 11.4 %all-to-all-done.3 = bf16[96,8,192]{0,1,2:T(8,128)(2,1)S(1)} async-done(((bf16[96,8,192]{0,1,2:T(8,128)(2,1)}), bf16[96,8,192]{0,1,2:T(8,128)(2,1)S(1)}, u32[]{:S(2)}, u32[]{:S(2)}) %all-to-all-start.3) | async-done | bytes 294944 | tf_op jit(solution)/shard_map/all_to_all | solution.py:53
  83.0 0.1 fusion.29
  83.1 0.0 copy-start.4
  83.1 0.1 multiply_reduce_fusion
  83.2 0.6 copy-done.4
  83.8 1.0 %fusion.14 = bf16[12,96,128]{2,1,0:T(8,128)(2,1)} fusion(f32[12,96,128]{2,1,0:T(8,128)S(1)} %fusion.11, f32[96,12]{0,1:T(8,128)S(1)} %add_rsqrt_fusion, f32[96,12]{0,1:T(8,128)S(1)} %broadcast_multiply_fusion, bf16[128,128]{1,0:T(8,128)(2,1)S(1)} %copy-done.4, bf16[96,8,16,12]{0,1,3,2:T(8,128)(2,1)S(1)} %bitcast.61), kind=kOutput, calls=%fused_computation.21 | convolution fusion | flops 38633472 | bytes 1221632 | tf_op jit(solution)/shard_map/jci,ce->ije/dot_general | solution.py:55
  (6 shorter events, 0.0 us)
Async XLA Ops:
  0.0 1.7 %copy-start = (bf16[128,128]{1,0:T(8,128)(2,1)S(1)}, bf16[128,128]{1,0:T(8,128)(2,1)}, u32[]{:S(2)}) copy-start(bf16[128,128]{1,0:T(8,128)(2,1)} %param.12) | copy-start | bytes 98308
  0.0 1.2 %copy-start.1 = (bf16[12,96,128]{2,1,0:T(8,128)(2,1)S(1)}, bf16[12,96,128]{2,1,0:T(8,128)(2,1)}, u32[]{:S(2)}) copy-start(bf16[12,96,128]{2,1,0:T(8,128)(2,1)} %param.8) | copy-start | bytes 884740
  1.7 0.8 copy-start.7
  2.5 0.8 copy-start.2
  5.0 7.6 %copy-start.5 = (bf16[128,128]{1,0:T(8,128)(2,1)S(1)}, bf16[128,128]{1,0:T(8,128)(2,1)}, u32[]{:S(2)}) copy-start(bf16[128,128]{1,0:T(8,128)(2,1)} %param.10) | copy-start | bytes 98308
  5.0 21.8 %all-to-all-start = ((bf16[128,12,96]{2,1,0:T(8,128)(2,1)}), bf16[128,12,96]{2,1,0:T(8,128)(2,1)S(1)}, u32[]{:S(2)}, u32[]{:S(2)}) async-start(bf16[128,12,96]{2,1,0:T(8,128)(2,1)} %copy.22), calls=%async_computation | async-start | bytes 1048576 | tf_op jit(solution)/shard_map/all_to_all | solution.py:43
  12.6 0.8 copy-start.3
  26.8 18.4 %all-to-all-start.2 = ((bf16[128,12,96]{2,1,0:T(8,128)(2,1)}), bf16[128,12,96]{2,1,0:T(8,128)(2,1)S(1)}, u32[]{:S(2)}, u32[]{:S(2)}) async-start(bf16[128,12,96]{2,1,0:T(8,128)(2,1)} %copy.27), calls=%async_computation.2 | async-start | bytes 1048576 | tf_op jit(solution)/shard_map/all_to_all | solution.py:42
  45.3 19.0 %all-to-all-start.1 = ((bf16[8,192,96]{2,0,1:T(8,128)(2,1)}), bf16[8,192,96]{2,0,1:T(8,128)(2,1)S(1)}, u32[]{:S(2)}, u32[]{:S(2)}) async-start(bf16[8,192,96]{2,0,1:T(8,128)(2,1)} %bitcast.7), calls=%async_computation.1 | async-start | bytes 786432 | tf_op jit(solution)/shard_map/all_to_all | solution.py:45
  66.2 4.6 %copy-start.6 = (bf16[128,128]{1,0:T(8,128)(2,1)S(1)}, bf16[128,128]{1,0:T(8,128)(2,1)}, u32[]{:S(2)}) copy-start(bf16[128,128]{1,0:T(8,128)(2,1)} %param.14) | copy-start | bytes 98308
  66.2 16.7 %all-to-all-start.3 = ((bf16[96,8,192]{0,1,2:T(8,128)(2,1)}), bf16[96,8,192]{0,1,2:T(8,128)(2,1)S(1)}, u32[]{:S(2)}, u32[]{:S(2)}) async-start(bf16[96,8,192]{0,1,2:T(8,128)(2,1)} %copy.32), calls=%async_computation.3 | async-start | bytes 786432 | tf_op jit(solution)/shard_map/all_to_all | solution.py:53
  83.1 0.8 copy-start.4
where the time goes:
time: 85.6 us; the launch traced here: 84.8 us
  waiting for transfers between devices  36.5 us (43%)
  starting transfers between devices  19.7 us (23%)
  blocking collectives  15 us (18%)
  local copies, waits for them, and re-layouts  6.45 us (8%)
  matrix products  4.94 us (6%)
  other arithmetic  1.92 us (2%)
    all_gather x1, blocking collectives, local(): lax.all_gather(left_rows, 'col', axis=2, tiled=True)  15 us
    all_to_all x1, waiting for transfers between devices, local(): lax.all_to_all(left, 'row', split_axis=0, concat_axis=1, tiled=True)  13.4 us
    all_to_all x1, waiting for transfers between devices, local(): lax.all_to_all(right, 'row', split_axis=0, concat_axis=1, tiled=True)  11.7 us
    all_to_all x1, waiting for transfers between devices, local(): lax.all_to_all(triangle, 'row', split_axis=2, concat_axis=1, tiled=True)  11.4 us
    all_to_all x1, starting transfers between devices, local(): lax.all_to_all(right, 'row', split_axis=0, concat_axis=1, tiled=True)  7.55 us
    all_to_all x1, starting transfers between devices, local(): lax.all_to_all(triangle, 'row', split_axis=2, concat_axis=1, tiled=True)  4.54 us
    all_to_all x1, starting transfers between devices, local(): lax.all_to_all(left, 'row', split_axis=0, concat_axis=1, tiled=True)  4.16 us
    all_to_all x1, starting transfers between devices, local(): lax.all_to_all(right_rows, 'col', split_axis=1, concat_axis=2, tiled=True)  3.47 us
  transfers between devices with their start and end apart: 4, of which 3 were waited for; matrix products, arithmetic and copies ran while one was open for 5% of the time, Pallas kernels for 0%

commit v1 on v0

--- a/solution.py
+++ b/solution.py
@@ -4,6 +4,13 @@
 from jax.sharding import PartitionSpec as P
 
 TILES = 12
+
+
+def exchange_blocks(x, axis, split, join):
+    size = lax.axis_size(axis)
+    tiles = jnp.stack(jnp.split(x, size, axis=split), axis=0)
+    tiles = lax.all_to_all(tiles, axis, split_axis=0, concat_axis=0)
+    return jnp.concatenate(tiles, axis=join)
 
 
 def norm_axis(values, axis):
@@ -40,7 +47,7 @@
     )
     left_rows, right_rows = (
         lax.all_to_all(left, "row", split_axis=0, concat_axis=1, tiled=True),
-        lax.all_to_all(right, "row", split_axis=0, concat_axis=1, tiled=True),
+        exchange_blocks(right, "row", 0, 1),
     )
     right_block = lax.all_to_all(right_rows, "col", split_axis=1, concat_axis=2, tiled=True)
     triangle = jnp.einsum(

time: 85.6 us -> 102 us (1.19)
  blocking collectives: 15 us -> 32.5 us
  local copies, waits for them, and re-layouts: 6.45 us -> 23.7 us
  waiting for transfers between devices: 36.5 us -> 21.8 us
  starting transfers between devices: 19.7 us -> 15.6 us
    all_to_all x0 -> x1, blocking collectives: none -> 17.5 us  [local(): lax.all_to_all(left, 'row', split_axis=0, concat_axis=1, tiled=True)]
    all_to_all x2 -> x1, waiting for transfers between devices: 25.2 us -> 10.4 us  [exchange_blocks(): tiles = lax.all_to_all(tiles, axis, split_axis=0, concat_axis=0)]
    another operation x0 -> x18, local copies, waits for them, and re-layouts: none -> 10.9 us  [exchange_blocks(): tiles = jnp.stack(jnp.split(x, size, axis=split), axis=0)]
    unnamed x16 -> x31, local copies, waits for them, and re-layouts: 1.08 us -> 10.2 us
    all_to_all x2 -> x1, starting transfers between devices: 11.7 us -> 7.59 us  [exchange_blocks(): tiles = lax.all_to_all(tiles, axis, split_axis=0, concat_axis=0)]
    convert_element_type x1 -> x0, local copies, waits for them, and re-layouts: 1.19 us -> none  [local(): (jax.nn.sigmoid(project(w_right_gate)) * project(w_right) * pair_mask[Non...]
  transfers between devices with their start and end apart: 4 -> 3, of which waited for: 3 -> 2; matrix products, arithmetic and copies ran while one was open for 5% -> 3% of each run, Pallas kernels for 0% -> 0%
where the time goes in v1:
time: 102 us; the launch traced here: 101 us
  blocking collectives  32.5 us (32%)
  local copies, waits for them, and re-layouts  23.7 us (23%)
  waiting for transfers between devices  21.8 us (21%)
  starting transfers between devices  15.6 us (15%)
  matrix products  4.94 us (5%)
  other arithmetic  1.95 us (2%)
    all_to_all x1, blocking collectives, local(): lax.all_to_all(left, 'row', split_axis=0, concat_axis=1, tiled=True)  17.5 us
    all_gather x1, blocking collectives, local(): lax.all_gather(left_rows, 'col', axis=2, tiled=True)  15 us
    all_to_all x1, waiting for transfers between devices, local(): lax.all_to_all(triangle, 'row', split_axis=2, concat_axis=1, tiled=True)  11.4 us
    another operation x18, local copies, waits for them, and re-layouts, exchange_blocks(): tiles = jnp.stack(jnp.split(x, size, axis=split), axis=0)  10.9 us
    all_to_all x1, waiting for transfers between devices, exchange_blocks(): tiles = lax.all_to_all(tiles, axis, split_axis=0, concat_axis=0)  10.4 us
    unnamed x31, local copies, waits for them, and re-layouts  10.2 us
    all_to_all x1, starting transfers between devices, exchange_blocks(): tiles = lax.all_to_all(tiles, axis, split_axis=0, concat_axis=0)  7.59 us
    all_to_all x1, starting transfers between devices, local(): lax.all_to_all(triangle, 'row', split_axis=2, concat_axis=1, tiled=True)  4.55 us
  transfers between devices with their start and end apart: 3, of which 2 were waited for; matrix products, arithmetic and copies ran while one was open for 3% of the time, Pallas kernels for 0%

profile of v1, /device:TPU:0, one launch (start us, length us, event | category | flops | bytes accessed | tf_op | source)
XLA Modules:
  0.0 100.8 jit_solution(6195479273498588201)
XLA Ops:
  0.0 1.2 %convert_reduce_fusion = f32[12,96]{1,0:T(8,128)S(1)} fusion(bf16[12,96,128]{2,1,0:T(8,128)(2,1)} %param.8), kind=kLoop, calls=%fused_computation.34 | loop fusion | flops 293760 | bytes 299520 | tf_op jit(solution)/shard_map/reduce_sum | solution.py:17
  1.2 0.5 fusion.26
  1.8 0.8 fusion.8
  2.6 0.3 fusion.18
  2.9 0.5 copy-done.2
  3.3 0.5 fusion.17
  3.9 2.4 %slice_bitcast_fusion = (bf16[1,8,12,96]{1,3,2,0:T(8,128)(2,1)S(1)}, bf16[1,8,12,96]{1,3,2,0:T(8,128)(2,1)S(1)}, bf16[1,8,12,96]{1,3,2,0:T(8,128)(2,1)S(1)}, bf1...) fusion(bf16[128,12,96]{0,2,1:T(8,128)(2,1)S(1)} %fusion.17), kind=kLoop, calls=%fused_computation.43 | loop fusion | bytes 589824 | tf_op jit(solution)/shard_map/stack | solution.py:11
  6.3 1.1 %copy.20 = bf16[1,8,12,96]{3,1,2,0:T(8,128)(2,1)S(1)} copy(bf16[1,8,12,96]{1,3,2,0:T(8,128)(2,1)} %get-tuple-element.20) | data formatting | bytes 36864 | tf_op jit(solution)/shard_map/stack | solution.py:11
  7.3 0.6 constant_dynamic-update-slice_fusion.15
  8.0 1.1 %copy.21 = bf16[1,8,12,96]{3,1,2,0:T(8,128)(2,1)S(1)} copy(bf16[1,8,12,96]{1,3,2,0:T(8,128)(2,1)} %get-tuple-element.19) | data formatting | bytes 36864 | tf_op jit(solution)/shard_map/stack | solution.py:11
  9.0 1.1 %copy.22 = bf16[1,8,12,96]{3,1,2,0:T(8,128)(2,1)S(1)} copy(bf16[1,8,12,96]{1,3,2,0:T(8,128)(2,1)} %get-tuple-element.18) | data formatting | bytes 36864 | tf_op jit(solution)/shard_map/stack | solution.py:11
  10.1 1.1 %copy.23 = bf16[1,8,12,96]{3,1,2,0:T(8,128)(2,1)S(1)} copy(bf16[1,8,12,96]{1,3,2,0:T(8,128)(2,1)} %get-tuple-element.17) | data formatting | bytes 36864 | tf_op jit(solution)/shard_map/stack | solution.py:11
  11.2 1.1 %copy.24 = bf16[1,8,12,96]{3,1,2,0:T(8,128)(2,1)S(1)} copy(bf16[1,8,12,96]{1,3,2,0:T(8,128)(2,1)} %get-tuple-element.16) | data formatting | bytes 36864 | tf_op jit(solution)/shard_map/stack | solution.py:11
  12.3 1.1 %copy.25 = bf16[1,8,12,96]{3,1,2,0:T(8,128)(2,1)S(1)} copy(bf16[1,8,12,96]{1,3,2,0:T(8,128)(2,1)} %get-tuple-element.15) | data formatting | bytes 36864 | tf_op jit(solution)/shard_map/stack | solution.py:11
  14.8 0.6 constant_dynamic-update-slice_fusion.14
  15.4 0.6 constant_dynamic-update-slice_fusion.13
  16.0 0.6 constant_dynamic-update-slice_fusion.12
  16.6 0.6 constant_dynamic-update-slice_fusion.11
  17.2 0.6 constant_dynamic-update-slice_fusion.10
  17.8 0.6 constant_dynamic-update-slice_fusion.9
  18.4 0.6 constant_dynamic-update-slice_fusion.8
  19.0 0.6 constant_dynamic-update-slice_fusion.7
  19.6 0.6 constant_dynamic-update-slice_fusion.6
  20.3 0.6 constant_dynamic-update-slice_fusion.5
  20.9 0.6 constant_dynamic-update-slice_fusion.4
  21.5 0.6 constant_dynamic-update-slice_fusion.3
  22.1 0.6 constant_dynamic-update-slice_fusion.2
  22.7 0.6 constant_dynamic-update-slice_fusion.1
  23.3 0.6 constant_dynamic-update-slice_fusion
  23.9 7.6 %all-to-all-start = ((bf16[16,8,12,96]{3,1,2,0:T(8,128)(2,1)}), bf16[16,8,12,96]{3,1,2,0:T(8,128)(2,1)}, u32[]{:S(2)}, u32[]{:S(2)}) async-start(bf16[16,8,12,96]{3,1,2,0:T(8,128)(2,1)} %constant_dynamic-update-slice_fusion), calls=%async_computation | async-start | bytes 786432 | tf_op jit(solution)/shard_map/all_to_all | solution.py:12
  31.5 0.8 fusion.5
  32.3 0.5 fusion.16
  32.8 0.4 copy.37
  33.3 10.4 %all-to-all-done = bf16[16,8,12,96]{3,1,2,0:T(8,128)(2,1)} async-done(((bf16[16,8,12,96]{3,1,2,0:T(8,128)(2,1)}), bf16[16,8,12,96]{3,1,2,0:T(8,128)(2,1)}, u32[]{:S(2)}, u32[]{:S(2)}) %all-to-all-start) | async-done | bytes 294944 | tf_op jit(solution)/shard_map/all_to_all | solution.py:12
  43.7 17.5 %all_to_all.50 = bf16[128,12,96]{2,1,0:T(8,128)(2,1)S(1)} all-to-all(bf16[128,12,96]{2,1,0:T(8,128)(2,1)S(1)} %copy.37), channel_id=1, replica_groups=mesh['row'=16,'col'=2] {'row'}, dimensions={0} | all-to-all | bytes 589824 | tf_op jit(solution)/shard_map/all_to_all | solution.py:49
  61.2 3.5 %all-to-all-start.1 = ((bf16[8,192,96]{2,0,1:T(8,128)(2,1)}), bf16[8,192,96]{2,0,1:T(8,128)(2,1)S(1)}, u32[]{:S(2)}, u32[]{:S(2)}) async-start(bf16[8,192,96]{2,0,1:T(8,128)(2,1)} %bitcast.21), calls=%async_computation.1 | async-start | bytes 786432 | tf_op jit(solution)/shard_map/all_to_all | solution.py:52
  64.8 0.4 copy.40
  65.2 15.0 %all_gather.3 = bf16[8,192,192]{1,0,2:T(8,128)(2,1)S(1)} all-gather(bf16[8,192,96]{1,0,2:T(8,128)(2,1)S(1)} %copy.40), channel_id=1, replica_groups=mesh['row'=16,'col'=2] {'col'}, dimensions={2}, use_global_device_ids=true | all-gather | bytes 884736 | tf_op jit(solution)/shard_map/all_gather | solution.py:55
  80.3 0.4 copy.52
  80.7 0.2 all_to_all.40
  80.9 0.3 fusion.15
  81.2 1.0 copy.42
  82.2 4.5 %all-to-all-start.3 = ((bf16[96,8,192]{0,1,2:T(8,128)(2,1)}), bf16[96,8,192]{0,1,2:T(8,128)(2,1)S(1)}, u32[]{:S(2)}, u32[]{:S(2)}) async-start(bf16[96,8,192]{0,1,2:T(8,128)(2,1)} %copy.42), calls=%async_computation.3 | async-start | bytes 786432 | tf_op jit(solution)/shard_map/all_to_all | solution.py:60
  86.7 0.8 fusion.11
  87.5 11.4 %all-to-all-done.3 = bf16[96,8,192]{0,1,2:T(8,128)(2,1)S(1)} async-done(((bf16[96,8,192]{0,1,2:T(8,128)(2,1)}), bf16[96,8,192]{0,1,2:T(8,128)(2,1)S(1)}, u32[]{:S(2)}, u32[]{:S(2)}) %all-to-all-start.3) | async-done | bytes 294944 | tf_op jit(solution)/shard_map/all_to_all | solution.py:60
  99.0 0.1 multiply_reduce_fusion
  99.2 0.6 copy-done.4
  99.8 1.0 fusion.14
  (33 shorter events, 1.7 us)
Async XLA Ops:
  0.0 1.8 %copy-start = (bf16[128,128]{1,0:T(8,128)(2,1)S(1)}, bf16[128,128]{1,0:T(8,128)(2,1)}, u32[]{:S(2)}) copy-start(bf16[128,128]{1,0:T(8,128)(2,1)} %param.12) | copy-start | bytes 98308
  0.0 1.2 %copy-start.1 = (bf16[12,96,128]{2,1,0:T(8,128)(2,1)S(1)}, bf16[12,96,128]{2,1,0:T(8,128)(2,1)}, u32[]{:S(2)}) copy-start(bf16[12,96,128]{2,1,0:T(8,128)(2,1)} %param.8) | copy-start | bytes 884740
  1.8 0.8 copy-start.7
  2.6 0.8 copy-start.2
  23.9 7.6 %copy-start.5 = (bf16[128,128]{1,0:T(8,128)(2,1)S(1)}, bf16[128,128]{1,0:T(8,128)(2,1)}, u32[]{:S(2)}) copy-start(bf16[128,128]{1,0:T(8,128)(2,1)} %param.10) | copy-start | bytes 98308
  23.9 19.8 %all-to-all-start = ((bf16[16,8,12,96]{3,1,2,0:T(8,128)(2,1)}), bf16[16,8,12,96]{3,1,2,0:T(8,128)(2,1)}, u32[]{:S(2)}, u32[]{:S(2)}) async-start(bf16[16,8,12,96]{3,1,2,0:T(8,128)(2,1)} %constant_dynamic-update-slice_fusion), calls=%async_computation | async-start | bytes 786432 | tf_op jit(solution)/shard_map/all_to_all | solution.py:12
  31.5 0.8 copy-start.3
  61.2 19.0 %all-to-all-start.1 = ((bf16[8,192,96]{2,0,1:T(8,128)(2,1)}), bf16[8,192,96]{2,0,1:T(8,128)(2,1)S(1)}, u32[]{:S(2)}, u32[]{:S(2)}) async-start(bf16[8,192,96]{2,0,1:T(8,128)(2,1)} %bitcast.21), calls=%async_computation.1 | async-start | bytes 786432 | tf_op jit(solution)/shard_map/all_to_all | solution.py:52
  82.2 4.6 %copy-start.6 = (bf16[128,128]{1,0:T(8,128)(2,1)S(1)}, bf16[128,128]{1,0:T(8,128)(2,1)}, u32[]{:S(2)}) copy-start(bf16[128,128]{1,0:T(8,128)(2,1)} %param.14) | copy-start | bytes 98308
  82.2 16.7 %all-to-all-start.3 = ((bf16[96,8,192]{0,1,2:T(8,128)(2,1)}), bf16[96,8,192]{0,1,2:T(8,128)(2,1)S(1)}, u32[]{:S(2)}, u32[]{:S(2)}) async-start(bf16[96,8,192]{0,1,2:T(8,128)(2,1)} %copy.42), calls=%async_computation.3 | async-start | bytes 786432 | tf_op jit(solution)/shard_map/all_to_all | solution.py:60
  99.0 0.8 copy-start.4
